TPU v7x, 256 devices: a whole 4x4x8 slice. The times are simulated.
256 devices in a mesh: grp: 32 (over y_hi, z, core), col: 8 (over x, y_lo).
Axes of the slice: x: 4, y: 4 (y_hi: 2, y_lo: 2; y = y_hi * 2 + y_lo), z: 8, core: 2. Of those that a mesh axis runs over, the one named last changes fastest.
Arguments:
- grad: float32 [4096, 16384], P('col', 'grp'), may hold values from -1.8 to 1.8
- exp_avg: float32 [4096, 16384], P('col', 'grp'), may hold values from -1.8 to 1.8
- exp_avg_sq: float32 [4096, 16384], P('col', 'grp'), may hold values from 0.01 to 0.36
- left_basis: bfloat16 [4096, 4096], P('grp', 'col'), may hold values from -1 to 1
- right_basis: bfloat16 [16384, 512], P('grp', 'col'), may hold values from -1 to 1
- gram_left: float32 [4096, 4096], P('grp', 'col'), may hold values from -6 to 6
- gram_right: float32 [16384, 512], P('grp', 'col'), may hold values from -6 to 6
Outputs:
- update: float32 [4096, 16384], P('col', 'grp')
- first_moment: float32 [4096, 16384], P('col', 'grp')
- second_moment: float32 [4096, 16384], P('col', 'grp')
- left_stat: float32 [4096, 4096], P('grp', 'col')
- right_stat: float32 [16384, 512], P('grp', 'col')
All inputs are finite; a program needn't handle non-finite values.
Results may differ from a plain program's by a relative error of at most 0.0041.
Values may be sent and summed in bfloat16 or wider, within the bound.
A program may use at most 128 MiB of HBM per device.

v0:
```python
import jax
import jax.numpy as jnp
from jax import lax
from jax.sharding import Mesh
from jax.sharding import PartitionSpec as P

RB = 512
GRP = ("grp_0", "grp_1", "grp_2")


decay = 0.95
bias_fix = 1.0 - decay**10


def in_order(pieces, dim):
    lengths = list(pieces.shape[1:])
    lengths[dim] *= pieces.shape[0]
    return jnp.moveaxis(pieces, 0, dim).reshape(lengths)


def copy_for_each(shard, axis):
    count = lax.axis_size(axis)
    return lax.all_to_all(
        jnp.broadcast_to(shard[None], (count, *shard.shape)), axis, 0, 0, tiled=True
    )


def gathered_copies(shard, axis, dim):
    return in_order(copy_for_each(shard, axis), dim)


def whole_of(shard, axes, dim):
    far, near = axes
    pieces = copy_for_each(copy_for_each(shard, far), near)
    return in_order(pieces.swapaxes(0, 1).reshape(-1, *shard.shape), dim)


def in_blocks(shard, dim, count):
    before, after = (shard.shape[:dim], shard.shape[dim + 1 :])
    return jnp.moveaxis(shard.reshape(*before, count, -1, *after), dim, 0)


def sum_at_owner(shard, axis, dim):
    count = lax.axis_size(axis)
    pieces = lax.all_to_all(in_blocks(shard, dim, count), axis, 0, 0, tiled=True)
    return jnp.sum(pieces, axis=0)


def sum_by_axis(shard, axes, dim):
    far, near = axes
    pieces = in_blocks(shard, dim, lax.axis_size(far))
    nearer = sum_at_owner(pieces, near, dim + 1)
    arrived = lax.all_to_all(nearer, far, split_axis=0, concat_axis=0, tiled=True)
    return arrived.sum(axis=0)


def local(grad, exp_avg, exp_avg_sq, left_basis, right_basis, gram_left, gram_right):
    col_count = lax.axis_size("col")
    rows_here, cols_here = grad.shape
    block_count = cols_here // RB
    rounded = grad.astype(jnp.bfloat16)
    panels = gathered_copies(right_basis, "col", 1)
    blocks = panels.reshape(block_count, RB, RB)
    gathered = lax.all_gather(rounded, "col", axis=0, tiled=True)
    height = gathered.shape[0]
    product = jnp.einsum(
        "mbj,bjr->mbr",
        gathered.reshape(height, block_count, RB),
        blocks,
        preferred_element_type=jnp.float32,
    )
    turned = product.reshape(height, cols_here).astype(jnp.bfloat16)
    left_cols = whole_of(left_basis, (("grp_0", "grp_1"), "grp_2"), 0)
    rotated = lax.dot_general(
        left_cols, turned, (((0,), (0,)), ((), ())), preferred_element_type=jnp.float32
    )
    first_moment = decay * exp_avg + (1.0 - decay) * rotated
    second_moment = decay * exp_avg_sq + (1.0 - decay) * rotated * rotated
    direction = (first_moment / bias_fix / (jnp.sqrt(second_moment / bias_fix) + 1e-08)).astype(
        jnp.bfloat16
    )
    left_rows = lax.all_to_all(left_cols, "col", split_axis=0, concat_axis=1, tiled=True)
    back = jnp.dot(
        left_rows,
        lax.all_gather(direction, "col", axis=0, tiled=True),
        preferred_element_type=jnp.float32,
    )
    back = back.astype(jnp.bfloat16)
    update = jnp.einsum(
        "mbr,bjr->mbj",
        back.reshape(rows_here, block_count, RB),
        blocks,
        preferred_element_type=jnp.float32,
    )
    update = update.reshape(rows_here, cols_here)
    left_term = sum_by_axis(
        lax.dot_general(
            gathered, rounded, (((1,), (1,)), ((), ())), preferred_element_type=jnp.float32
        ),
        (("grp_0", "grp_1"), "grp_2"),
        0,
    )
    left_stat = decay * gram_left + (1.0 - decay) * left_term
    share = RB // col_count
    offset = lax.axis_index("col") * share
    whole_blocks = gathered.reshape(gathered.shape[0], block_count, RB)
    narrow = lax.dynamic_slice_in_dim(whole_blocks, offset, share, 2)
    right_term = jnp.einsum(
        "mbj,mbr->bjr", whole_blocks, narrow, preferred_element_type=jnp.float32
    )
    right_stat = decay * gram_right + (1.0 - decay) * right_term.reshape(cols_here, share)
    return (update, first_moment, second_moment, left_stat, right_stat)


def solution(mesh):
    finer = Mesh(
        mesh.devices.reshape(2, 8, 2, mesh.shape["col"]), ("grp_0", "grp_1", "grp_2", "col")
    )
    placed = (
        P("col", GRP),
        P("col", GRP),
        P("col", GRP),
        P(GRP, "col"),
        P(GRP, "col"),
        P(GRP, "col"),
        P(GRP, "col"),
    )
    return jax.shard_map(
        local,
        mesh=finer,
        in_specs=placed,
        out_specs=(P("col", GRP), P("col", GRP), P("col", GRP), P(GRP, "col"), P(GRP, "col")),
        check_vma=False,
    )
```

profile of v0, /device:TPU:4, one launch (start us, length us, event | category | flops | bytes accessed | tf_op | source)
XLA Modules:
  0.0 361.9 jit_solution(3152248950246105111)
XLA Ops:
  7.2 0.0 all-gather.3.cloned.1.call-start
  7.2 2.1 convert_element_type.22
  9.3 0.0 all-gather.3.cloned.1.call-update
  9.3 1.1 broadcast_in_dim.7
  10.4 62.0 %all_to_all.44 = bf16[16,128,512]{2,1,0:T(8,128)(2,1)S(1)} all-to-all(bf16[16,128,512]{2,1,0:T(8,128)(2,1)S(1)} %broadcast_in_dim.7), channel_id=1, replica_groups=mesh['grp_0'=2,'grp_1'=8,'grp_2'=2,'col'=8] {'grp_0','grp_1'}, dimensions={0} | all-to-all | bytes 4194304 | tf_op jit(solution)/shard_map/all_to_all | solution.py:23
  72.4 0.6 broadcast_in_dim.8
  73.0 0.0 copy-start.7
  73.0 8.3 %all_to_all.45 = bf16[2,16,128,512]{3,2,1,0:T(8,128)(2,1)} all-to-all(bf16[2,16,128,512]{3,2,1,0:T(8,128)(2,1)S(1)} %broadcast_in_dim.8), channel_id=1, replica_groups=mesh['grp_0'=2,'grp_1'=8,'grp_2'=2,'col'=8] {'grp_2'}, dimensions={0} | all-to-all | bytes 8388608 | tf_op jit(solution)/shard_map/all_to_all | solution.py:23
  81.3 0.8 broadcast_in_dim.6
  82.1 5.1 %all-to-all-start = ((bf16[8,512,64]{1,2,0:T(8,128)(2,1)}), bf16[8,512,64]{1,2,0:T(8,128)(2,1)S(1)}, u32[]{:S(2)}, u32[]{:S(2)}) async-start(bf16[8,512,64]{1,2,0:T(8,128)(2,1)} %broadcast_in_dim.6), calls=%async_computation | async-start | bytes 1048576 | tf_op jit(solution)/shard_map/all_to_all | solution.py:23
  87.2 4.7 %copy.30 = bf16[2,16,128,512]{3,2,0,1:T(8,128)(2,1)} copy(bf16[2,16,128,512]{3,2,1,0:T(8,128)(2,1)} %all_to_all.45) | data formatting | bytes 8388608 | tf_op jit(solution)/shard_map/all_to_all | solution.py:23
  91.9 38.2 %all-gather.3.cloned.1.call-done = bf16[4096,512]{1,0:T(8,128)(2,1)} async-done(((bf16[512,512]{1,0:T(8,128)(2,1)}), bf16[4096,512]{1,0:T(8,128)(2,1)}) %all-gather.3.cloned.1.call-update) | async-done | bytes 4194320 | tf_op jit(solution)/shard_map/all_gather | solution.py:64
  130.1 4.8 %fusion.8 = f32[4096,512]{1,0:T(8,128)S(1)} fusion(bf16[4096,512]{1,0:T(8,128)(2,1)} %all-gather.3.cloned.1.call-done, bf16[512,512]{1,0:T(8,128)(2,1)S(1)} %copy-done), kind=kOutput, calls=%fused_computation.16 | convolution fusion | flops 2147483648 | bytes 13107200 | tf_op jit(solution)/shard_map/dot_general | solution.py:97
  134.8 4.2 %copy.37 = f32[16,2,128,512]{3,2,0,1:T(8,128)} copy(f32[16,2,128,512]{3,2,1,0:T(8,128)S(1)} %bitcast.39) | data formatting | bytes 16777216 | tf_op jit(solution)/shard_map/reshape;reshape | solution.py:40
  139.1 18.5 %all_to_all.46 = f32[2,16,128,512]{3,2,1,0:T(8,128)} all-to-all(f32[2,16,128,512]{3,2,1,0:T(8,128)} %bitcast.40), channel_id=1, replica_groups=mesh['grp_0'=2,'grp_1'=8,'grp_2'=2,'col'=8] {'grp_2'}, dimensions={0} | all-to-all | bytes 16777216 | tf_op jit(solution)/shard_map/all_to_all | solution.py:45
  157.6 5.6 %all-to-all-start.3 = ((bf16[8,512,512]{2,1,0:T(8,128)(2,1)}), bf16[8,512,512]{2,1,0:T(8,128)(2,1)}, u32[]{:S(2)}, u32[]{:S(2)}) async-start(bf16[8,512,512]{2,1,0:T(8,128)(2,1)} %bitcast.41), calls=%async_computation.3 | async-start | bytes 8388608 | tf_op jit(solution)/shard_map/all_to_all | solution.py:82
  163.2 0.3 copy.29
  163.5 1.3 copy.31
  164.8 9.8 %divide_convert_fusion = (bf16[512,512]{0,1:T(8,128)(2,1)}, f32[512,512]{0,1:T(8,128)S(1)}, f32[512,512]{0,1:T(8,128)S(1)}) fusion(f32[512,512]{0,1:T(8,128)S(1)} %copy.29, f32[512,512]{0,1:T(8,128)} %copy.31, bf16[4096,512]{1,0:T(8,128)(2,1)} %bitcast.42, bf16[512,512]{0,1:T(8,128)(2,1)} %bitcast.44, bf16[4096,512]{1,0:T(8,128)(2,1)} %all-gather.3.cloned.1.call-done), kind=kOutput, calls=%fused_computation.13 | convolution fusion | flops 4299948032 | bytes 13631488 | tf_op jit(solution)/shard_map/dot_general | solution.py:74
  174.6 0.0 all-gather.5.cloned.1.call-update
  174.6 6.8 %reduce_sum.18 = f32[16,128,512]{2,1,0:T(8,128)} reduce(f32[2,16,128,512]{3,2,1,0:T(8,128)} %all_to_all.46, f32[]{:T(128)} %constant.13.clone.1), dimensions={0}, to_apply=%region_0.0 | reduce | flops 1048576 | bytes 12582916 | tf_op jit(solution)/shard_map/reduce_sum | solution.py:46
  181.4 39.9 %all-to-all-done.3 = bf16[8,512,512]{2,1,0:T(8,128)(2,1)} async-done(((bf16[8,512,512]{2,1,0:T(8,128)(2,1)}), bf16[8,512,512]{2,1,0:T(8,128)(2,1)}, u32[]{:S(2)}, u32[]{:S(2)}) %all-to-all-start.3) | async-done | bytes 4194336 | tf_op jit(solution)/shard_map/all_to_all | solution.py:82
  221.3 10.7 %all-to-all-start.5 = ((f32[16,128,512]{2,1,0:T(8,128)}), f32[16,128,512]{2,1,0:T(8,128)}, u32[]{:S(2)}, u32[]{:S(2)}) async-start(f32[16,128,512]{2,1,0:T(8,128)} %reduce_sum.18), calls=%async_computation.5 | async-start | bytes 8388608 | tf_op jit(solution)/shard_map/all_to_all | solution.py:53
  232.0 0.0 copy-start.6
  232.0 1.3 copy.34
  233.3 1.3 copy.35
  234.6 4.5 %fusion.2 = f32[512,64]{0,1:T(8,128)} fusion(bf16[4096,512]{1,0:T(8,128)(2,1)} %all-gather.3.cloned.1.call-done, s32[]{:T(128)S(6)} %select_n.3, f32[512,64]{0,1:T(8,128)S(1)} %copy-done.6), kind=kOutput, calls=%fused_computation.9 | convolution fusion | flops 268533760 | bytes 5505028 | tf_op jit(solution)/shard_map/mbj,mbr->bjr/dot_general | solution.py:108
  239.1 6.5 %copy.32 = bf16[512,8,512]{0,2,1:T(8,128)(2,1)} copy(bf16[512,8,512]{2,0,1:T(8,128)(2,1)} %bitcast.9) | data formatting | bytes 8388608 | tf_op jit(solution)/shard_map/all_to_all | solution.py:82
  245.6 98.9 %all-gather.5.cloned.1.call-done = bf16[4096,512]{0,1:T(8,128)(2,1)} async-done(((bf16[512,512]{0,1:T(8,128)(2,1)}), bf16[4096,512]{0,1:T(8,128)(2,1)}) %all-gather.5.cloned.1.call-update) | async-done | bytes 4194320 | tf_op jit(solution)/shard_map/all_gather | solution.py:85
  344.5 7.1 %fusion.3 = f32[512,512]{1,0:T(8,128)} fusion(bf16[512,512]{0,1:T(8,128)(2,1)S(1)} %bitcast.45, bf16[4096,512]{0,1:T(8,128)(2,1)} %all-gather.5.cloned.1.call-done, bf16[512,4096]{0,1:T(8,128)(2,1)} %bitcast.43), kind=kOutput, calls=%fused_computation.10 | convolution fusion | flops 2416181248 | bytes 9961472 | tf_op jit(solution)/shard_map/mbr,bjr->mbj/dot_general | solution.py:89
  351.6 2.7 reduce_sum.19
  354.3 0.8 multiply_add_fusion.1
  (17 shorter events, 0.0 us)
Async XLA Ops:
  7.2 122.9 %all-gather.3.cloned.1.call-start = ((), (), s32[]{:S(2)}) async-start(), calls=%async_computation.6 | async-start | bytes 4718592 | tf_op jit(solution)/shard_map/all_gather | solution.py:64
  73.0 8.3 %copy-start.7 = (bf16[512,64]{0,1:T(8,128)(2,1)S(1)}, bf16[512,64]{0,1:T(8,128)(2,1)}, u32[]{:S(2)}) copy-start(bf16[512,64]{0,1:T(8,128)(2,1)} %param.11) | copy-start | bytes 196612
  82.1 57.0 %all-to-all-start = ((bf16[8,512,64]{1,2,0:T(8,128)(2,1)}), bf16[8,512,64]{1,2,0:T(8,128)(2,1)S(1)}, u32[]{:S(2)}, u32[]{:S(2)}) async-start(bf16[8,512,64]{1,2,0:T(8,128)(2,1)} %broadcast_in_dim.6), calls=%async_computation | async-start | bytes 1048576 | tf_op jit(solution)/shard_map/all_to_all | solution.py:23
  87.2 42.9 %copy-start = (bf16[512,512]{1,0:T(8,128)(2,1)S(1)}, bf16[512,512]{1,0:T(8,128)(2,1)}, u32[]{:S(2)}) copy-start(bf16[512,512]{1,0:T(8,128)(2,1)} %convert_element_type.22) | copy-start | bytes 1572868
  139.1 18.5 %copy-start.3 = (bf16[8,512,64]{1,2,0:T(8,128)(2,1)}, bf16[8,512,64]{1,2,0:T(8,128)(2,1)S(1)}, u32[]{:S(2)}) copy-start(bf16[8,512,64]{1,2,0:T(8,128)(2,1)S(1)} %all-to-all-done) | copy-start | bytes 1572868
  157.6 5.6 %copy-start.1 = (f32[512,512]{1,0:T(8,128)S(1)}, f32[512,512]{1,0:T(8,128)}, u32[]{:S(2)}) copy-start(f32[512,512]{1,0:T(8,128)} %param.8) | copy-start | bytes 3145732
  157.6 5.9 %copy-start.2 = (f32[512,512]{1,0:T(8,128)S(1)}, f32[512,512]{1,0:T(8,128)}, u32[]{:S(2)}) copy-start(f32[512,512]{1,0:T(8,128)} %param.9) | copy-start | bytes 3145732
  157.6 63.7 %all-to-all-start.3 = ((bf16[8,512,512]{2,1,0:T(8,128)(2,1)}), bf16[8,512,512]{2,1,0:T(8,128)(2,1)}, u32[]{:S(2)}, u32[]{:S(2)}) async-start(bf16[8,512,512]{2,1,0:T(8,128)(2,1)} %bitcast.41), calls=%async_computation.3 | async-start | bytes 8388608 | tf_op jit(solution)/shard_map/all_to_all | solution.py:82
  163.2 181.3 %all-gather.5.cloned.1.call-start = ((), (), s32[]{:S(2)}) async-start(), calls=%async_computation.7 | async-start | bytes 4718592 | tf_op jit(solution)/shard_map/all_gather | solution.py:85
  221.3 130.3 %all-to-all-start.5 = ((f32[16,128,512]{2,1,0:T(8,128)}), f32[16,128,512]{2,1,0:T(8,128)}, u32[]{:S(2)}, u32[]{:S(2)}) async-start(f32[16,128,512]{2,1,0:T(8,128)} %reduce_sum.18), calls=%async_computation.5 | async-start | bytes 8388608 | tf_op jit(solution)/shard_map/all_to_all | solution.py:53
  232.0 2.6 copy-start.6
  239.1 105.4 %copy-start.4 = (bf16[8,512,64]{1,2,0:T(8,128)(2,1)S(1)}, bf16[8,512,64]{1,2,0:T(8,128)(2,1)}, u32[]{:S(2)}) copy-start(bf16[8,512,64]{1,2,0:T(8,128)(2,1)} %copy-done.3) | copy-start | bytes 1572868
  351.6 2.7 copy-start.5
Sparse Core Ops, SparseCore 0:
  10.3 119.6 all-gather.2
  174.7 169.6 all-gather.4
where the time goes:
time: 364 us; the launch traced here: 362 us
  waiting for transfers between devices  177 us (49%)
  blocking collectives  88.7 us (24%)
  matrix products  26.1 us (7%)
  local copies, waits for them, and re-layouts  22.3 us (6%)
  starting transfers between devices  21.4 us (6%)
  between operations  14.1 us (4%)
  other arithmetic  12.3 us (3%)
    all_gather x1, waiting for transfers between devices, local(): lax.all_gather(direction, 'col', axis=0, tiled=True)  98.9 us
    all_to_all x2, blocking collectives, copy_for_each(): lax.all_to_all(jnp.broadcast_to(shard[None], (count, *shard.shape)), axis...  70.2 us
    all_to_all x1, waiting for transfers between devices, local(): lax.all_to_all(left_cols, 'col', split_axis=0, concat_axis=1, tiled=True)  39.9 us
    all_gather x1, waiting for transfers between devices, local(): gathered = lax.all_gather(rounded, 'col', axis=0, tiled=True)  38.2 us
    all_to_all x1, blocking collectives, sum_at_owner(): lax.all_to_all(in_blocks(shard, dim, count), axis, 0, 0, tiled=True)  18.5 us
    all_to_all x1, starting transfers between devices, sum_by_axis(): lax.all_to_all(nearer, far, split_axis=0, concat_axis=0, tiled=True)  10.7 us
    dot_general x1, matrix products, local(): lax.dot_general(left_cols, turned, (((0,), (0,)), ((), ())), preferred_el...  9.76 us
  transfers between devices with their start and end apart: 5, of which 3 were waited for; matrix products, arithmetic and copies ran while one was open for 15% of the time, Pallas kernels for 0%

commit v1 on v0

v1 whole, which is shorter than its diff:
```python
import functools

import jax
import jax.numpy as jnp
from jax import lax
from jax.experimental import pallas as pl
from jax.experimental.pallas import tpu as pltpu
from jax.sharding import PartitionSpec as P

decay = 0.95
bias_fix = 1.0 - decay**10
B16 = jnp.bfloat16
F32 = jnp.float32
BY_ROWS = (((1,), (1,)), ((), ()))
PLAIN = (((1,), (0,)), ((), ()))


def dot(a, b, dims=PLAIN):
    return lax.dot_general(a, b, dims, preferred_element_type=F32)


def kernel(
    grad, exp_avg, exp_avg_sq, left, right_t, gram_left, gram_right,
    update, first, second, left_stat, right_stat,
    G, R, L, LT, T, LP, EP, rot, right_acc, dirn,
    ER, ES, AO, YB, D1, D1Y, D2, D2Y, D3, S1, S1Y, S2, S2Y, S3,
    send_sem, g_sem, r_sem, l_sem, e_sem, er_sem, yb_sem, d1_sem, d1y_sem, d2_sem, d2y_sem, d3_sem,
):
    grp = lax.axis_index("grp")
    col = lax.axis_index("col")
    core = grp % 2
    z = (grp // 2) % 8
    yh = grp // 16
    x = col // 2
    yl = col % 2

    def z_at(k, half=None, c=None):
        h = yh if half is None else half
        cc = core if c is None else c
        return h * 16 + ((z + k + 8) % 8) * 2 + cc

    def c_at(k, flip=0):
        return ((x + k + 4) % 4) * 2 + (yl if flip == 0 else 1 - yl)

    oh = 1 - yh
    oc = 1 - core
    XP = {"grp": grp, "col": c_at(1)}
    XM = {"grp": grp, "col": c_at(-1)}
    YN = {"grp": grp, "col": c_at(0, 1)}
    ZP = {"grp": z_at(1), "col": col}
    ZM = {"grp": z_at(-1), "col": col}
    YF = {"grp": z_at(0, oh), "col": col}
    CO = {"grp": z_at(0, None, oc), "col": col}

    sends = []

    def send(src, dst, sem, to):
        cp = pltpu.make_async_remote_copy(
            src_ref=src, dst_ref=dst, send_sem=send_sem.at[len(sends)], recv_sem=sem,
            device_id=to, device_id_type=pl.DeviceIdType.MESH,
        )
        cp.start()
        sends.append(cp)

    def arrived(dst, sem):
        pltpu.make_async_remote_copy(
            src_ref=dst, dst_ref=dst, send_sem=send_sem.at[0], recv_sem=sem,
            device_id=XP, device_id_type=pl.DeviceIdType.MESH,
        ).wait_recv()

    H = G.shape[1] // 2
    W = R.shape[1] // 2

    def g_half(s, h):
        return G.at[s, pl.ds(h * H, H)]

    def r_half(s, h):
        return R.at[s, pl.ds(h * W, W)]

    def send_g(s, h, to):
        send(g_half(s, h), g_half(s, h), g_sem.at[s, h], to)

    def send_r(s, h, to):
        send(r_half(s, h), r_half(s, h), r_sem.at[s, h], to)

    def got_g(s, h):
        arrived(g_half(s, h), g_sem.at[s, h])

    def got_r(s, h):
        arrived(r_half(s, h), r_sem.at[s, h])

    def send_l(g, to):
        send(L.at[g], L.at[g], l_sem.at[g], to)

    def got_l(g):
        arrived(L.at[g], l_sem.at[g])

    G[col] = grad[...].astype(B16)
    R[col] = right_t[...]
    L[grp] = left[...]
    right_acc[...] = jnp.zeros_like(right_acc)
    rot[...] = jnp.zeros_like(rot)
    barrier = pltpu.get_barrier_semaphore()
    for to in (XP, XM, YN, ZP, ZM, YF, CO):
        pl.semaphore_signal(barrier, inc=1, device_id=to, device_id_type=pl.DeviceIdType.MESH)
    pl.semaphore_wait(barrier, 7)

    me = col
    xm, xp, yn = c_at(-1), c_at(1), c_at(0, 1)
    far = c_at(2)
    xm_n, xp_n, far_n = c_at(-1, 1), c_at(1, 1), c_at(2, 1)

    for h in (0, 1):
        for to in (YN, XP, XM):
            send_r(me, h, to)
    for to in (YF, ZP, ZM, CO):
        send_l(grp, to)
    for to in (YN, XP, XM):
        send_g(me, 0, to)

    def l_pass(g, to):
        got_l(g)
        if to is not None:
            send_l(g, to)
        send_l(g, CO)

    for h in (0, 1):
        got_r(xm, h)
        if h == 0:
            send_r(xm, 0, XP)
        got_r(xp, h)
        if h == 1:
            send_r(xp, 1, XM)
        got_r(yn, h)
        send_r(yn, h, XP)
        send_r(yn, h, XM)
    for to in (YN, XP, XM):
        send_g(me, 1, to)
    g = z_at(0, oh)
    got_l(g)
    send_l(g, ZP)
    send_l(g, ZM)
    send_l(g, CO)
    l_pass(z_at(-1), ZP)
    l_pass(z_at(1), ZM)
    l_pass(z_at(-1, oh), ZP)
    l_pass(z_at(1, oh), ZM)

    got_g(xm, 0)
    send_g(xm, 0, XP)
    got_g(yn, 0)
    send_g(yn, 0, XP)
    send_g(yn, 0, XM)
    got_g(xp, 0)
    got_r(far, 0)
    send_r(far, 0, YN)
    got_r(far, 1)
    send_r(far, 1, YN)

    l_pass(z_at(-2), ZP)
    l_pass(z_at(2), ZM)
    l_pass(z_at(-2, oh), ZP)
    l_pass(z_at(2, oh), ZM)

    got_g(xp, 1)
    send_g(xp, 1, XM)
    got_g(yn, 1)
    send_g(yn, 1, XP)
    send_g(yn, 1, XM)
    got_g(xm, 1)

    l_pass(z_at(-3), ZP)
    l_pass(z_at(3), None)
    l_pass(z_at(-3, oh), None)
    l_pass(z_at(3, oh), ZM)

    for s in (xm_n, xp_n, far_n):
        got_r(s, 0)
        got_r(s, 1)

    width = right_stat.shape[1]
    RB = G.shape[2]
    picks = lax.broadcasted_iota(jnp.int32, (128, RB), 0)
    lanes = lax.broadcasted_iota(jnp.int32, (128, RB), 1)
    chosen = jnp.where(
        jnp.logical_and(picks < width, lanes == picks + col * width), 1.0, 0.0
    ).astype(B16)

    def piece(s):
        rows = G[s]
        T[s] = dot(rows, R[...].reshape(RB, RB), BY_ROWS).astype(B16)
        LP[pl.ds(2 * s, 2)] = dot(rows, G[me], BY_ROWS).reshape(2, 2, 128, RB)
        narrow = dot(chosen, rows, BY_ROWS).astype(B16)
        right_acc[...] += dot(narrow, rows)

    def pair_send(s):
        send(
            LP.at[pl.ds(2 * s, 2), oc], EP.at[pl.ds(2 * s, 2)], e_sem.at[s], CO
        )

    def near_piece(i, carry):
        dx = jnp.where(i == 1, 3, jnp.where(i == 2, 1, 0))
        y = jnp.where(i == 3, 1 - yl, yl)
        piece(((x + dx) % 4) * 2 + y)
        return carry

    lax.fori_loop(0, 4, near_piece, 0)
    for s in (me, xm, xp, yn):
        pair_send(s)

    got_g(far, 0)
    send_g(far, 0, YN)
    got_g(far, 1)
    send_g(far, 1, YN)
    l_pass(z_at(4), None)
    l_pass(z_at(4, oh), None)
    for h in (yh, oh):
        for k in range(8):
            got_l(z_at(k, h, oc))

    def turn_left(r, carry):
        block = L[pl.ds(4 * r, 4)].reshape(RB, RB)
        LT[r] = block.T
        return carry

    lax.fori_loop(0, 8, turn_left, 0)

    for s in (xm_n, xp_n):
        got_g(s, 0)
        got_g(s, 1)
    got_g(far_n, 0)
    got_g(far_n, 1)

    def far_piece(i, carry):
        dx = jnp.where(i == 1, 3, jnp.where(i == 2, 1, 2))
        y = jnp.where(i == 0, yl, 1 - yl)
        piece(((x + dx) % 4) * 2 + y)
        return carry

    lax.fori_loop(0, 4, far_piece, 0)
    for s in (far, xm_n, xp_n, far_n):
        pair_send(s)

    def rotate(r, carry):
        rot[...] += dot(LT[r], T[r])
        return carry

    lax.fori_loop(0, 8, rotate, 0)

    def moments(i, carry):
        at = pl.ds(i * 64, 64)
        turned = rot[at, :]
        m1 = decay * exp_avg[at, :] + (1.0 - decay) * turned
        m2 = decay * exp_avg_sq[at, :] + (1.0 - decay) * turned * turned
        first[at, :] = m1
        second[at, :] = m2
        dirn[at, :] = (m1 / bias_fix / (jnp.sqrt(m2 / bias_fix) + 1e-08)).astype(B16)
        return carry

    lax.fori_loop(0, RB // 64, moments, 0)

    def back_of(d):
        return dot(L[pl.ds(4 * d, 4)].reshape(RB, RB), dirn[...])

    def half_of(d, h):
        block = L[pl.ds(4 * d, 4)].reshape(RB, RB)[h * H : (h + 1) * H]
        return dot(block, dirn[...])

    S1Y[...] = back_of(far_n).astype(B16)
    S1[0] = back_of(xp_n).astype(B16)
    S1[1] = back_of(xm_n).astype(B16)
    rows = [pl.ds(0, H), pl.ds(H, H)]
    for h in (0, 1):
        send(S1Y.at[rows[h]], D1Y.at[rows[h]], d1y_sem.at[h], YN)
    send(S1.at[0], D1.at[0], d1_sem.at[0], XP)
    send(S1.at[1], D1.at[1], d1_sem.at[1], XM)

    for s in (me, xm, xp, yn, far, xm_n, xp_n, far_n):
        arrived(EP.at[pl.ds(2 * s, 2)], e_sem.at[s])

    def stat_of(half, k):
        b = half * 8 + (z + k + 8) % 8
        return LP[b, core] + EP[b]

    def stat_step(step):
        for d in (0, 1):
            for k, half in ((0, yh), (1, oh)):
                length = 4 if d == k else 3
                if step > length:
                    continue
                away = length + 1 - step
                total = stat_of(half, away if d == 0 else -away)
                if step > 1:
                    arrived(ER.at[d, k, step - 2], er_sem.at[d, k, step - 2])
                    total = total + ER[d, k, step - 2].astype(F32)
                ES[d, k, step - 1] = total.astype(B16)
                send(
                    ES.at[d, k, step - 1], ER.at[d, k, step - 1],
                    er_sem.at[d, k, step - 1], ZP if d == 0 else ZM,
                )

    def stat_total(k):
        total = stat_of(yh if k == 0 else oh, 0)
        for d in (0, 1):
            last = 3 if d == k else 2
            arrived(ER.at[d, k, last], er_sem.at[d, k, last])
            total = total + ER[d, k, last].astype(F32)
        return total

    stat_step(1)
    S3[0, rows[1]] = half_of(xp, 1).astype(B16)
    S3[1, rows[0]] = half_of(xm, 0).astype(B16)

    arrived(D1Y.at[rows[0]], d1y_sem.at[0])
    S2[0] = (half_of(far, 0) + D1Y[rows[0]].astype(F32)).astype(B16)
    send(S2.at[0], D2.at[0], d2_sem.at[0], XP)
    send(S3.at[0, rows[1]], D3.at[0, rows[1]], d3_sem.at[0, 1], XP)
    send(S3.at[1, rows[0]], D3.at[1, rows[0]], d3_sem.at[1, 0], XM)

    stat_step(2)
    arrived(D1Y.at[rows[1]], d1y_sem.at[1])
    S2[1] = (half_of(far, 1) + D1Y[rows[1]].astype(F32)).astype(B16)
    send(S2.at[1], D2.at[1], d2_sem.at[1], XM)
    arrived(D1.at[0], d1_sem.at[0])
    arrived(D1.at[1], d1_sem.at[1])
    S2Y[...] = (back_of(yn) + D1[0].astype(F32) + D1[1].astype(F32)).astype(B16)
    send(S2Y, D2Y, d2y_sem.at[0], YN)

    stat_step(3)
    right_stat[...] = decay * gram_right[...] + (1.0 - decay) * right_acc[...].T[:, :width]
    arrived(D2.at[0], d2_sem.at[0])
    S3[0, rows[0]] = (half_of(xp, 0) + D2[0].astype(F32)).astype(B16)
    send(S3.at[0, rows[0]], D3.at[0, rows[0]], d3_sem.at[0, 0], XP)
    arrived(D2.at[1], d2_sem.at[1])
    S3[1, rows[1]] = (half_of(xm, 1) + D2[1].astype(F32)).astype(B16)
    send(S3.at[1, rows[1]], D3.at[1, rows[1]], d3_sem.at[1, 1], XM)
    stat_step(4)
    AO[...] = stat_total(1).astype(B16)
    send(AO, YB, yb_sem.at[0], YF)
    left_stat[...] = decay * gram_left[...] + (1.0 - decay) * stat_total(0)

    rot[...] = back_of(me)
    arrived(D2Y, d2y_sem.at[0])
    for h in (0, 1):
        for d in (0, 1):
            arrived(D3.at[d, rows[h]], d3_sem.at[d, h])
    back = rot[...] + D2Y[...].astype(F32) + (D3[0].astype(F32) + D3[1].astype(F32))
    update[...] = dot(back.astype(B16), R[...].reshape(RB, RB))
    arrived(YB, yb_sem.at[0])
    left_stat[...] += (1.0 - decay) * YB[...].astype(F32)
    for cp in sends:
        cp.wait_send()


def local(grad, exp_avg, exp_avg_sq, left_basis, right_basis, gram_left, gram_right):
    rows, RB = grad.shape
    assert rows == RB
    H = RB // 2
    width = right_basis.shape[1]
    vm = pltpu.VMEM
    dma = pltpu.SemaphoreType.DMA
    scratch = [
        vm((8, RB, RB), B16),
        vm((8, width, RB), B16),
        vm((32, 128, RB), B16),
        vm((8, RB, RB), B16),
        vm((8, RB, RB), B16),
        vm((16, 2, 128, RB), F32),
        vm((16, 128, RB), F32),
        vm((RB, RB), F32),
        vm((128, RB), F32),
        vm((RB, RB), B16),
        vm((2, 2, 4, 128, RB), B16),
        vm((2, 2, 4, 128, RB), B16),
        vm((128, RB), B16),
        vm((128, RB), B16),
        vm((2, RB, RB), B16),
        vm((RB, RB), B16),
        vm((2, H, RB), B16),
        vm((RB, RB), B16),
        vm((2, RB, RB), B16),
        vm((2, RB, RB), B16),
        vm((RB, RB), B16),
        vm((2, H, RB), B16),
        vm((RB, RB), B16),
        vm((2, RB, RB), B16),
        dma((128,)), dma((8, 2)), dma((8, 2)), dma((32,)), dma((8,)), dma((2, 2, 4)),
        dma((1,)), dma((2,)), dma((2,)), dma((2,)), dma((1,)), dma((2, 2)),
    ]
    whole = pl.BlockSpec(memory_space=pltpu.VMEM)
    like = lambda a: jax.ShapeDtypeStruct(a.shape, F32)
    return pl.pallas_call(
        kernel,
        out_shape=(like(grad), like(grad), like(grad), like(gram_left), like(gram_right)),
        in_specs=[whole] * 7,
        out_specs=(whole,) * 5,
        scratch_shapes=scratch,
        compiler_params=pltpu.CompilerParams(
            collective_id=0, has_side_effects=True, vmem_limit_bytes=64 * 1024 * 1024 - 65536
        ),
    )(grad, exp_avg, exp_avg_sq, left_basis, right_basis.T, gram_left, gram_right)


def solution(mesh):
    a, b = P("col", "grp"), P("grp", "col")
    return jax.shard_map(
        local, mesh=mesh, in_specs=(a, a, a, b, b, b, b), out_specs=(a, a, a, b, b), check_vma=False
    )
```

time: 364 us -> 102 us (0.28)
  waiting for transfers between devices: 177 us -> 0 us
  Pallas kernels: 0 us -> 92.2 us
  blocking collectives: 88.7 us -> 0 us
  matrix products: 26.1 us -> 0 us
  starting transfers between devices: 21.4 us -> 0 us
  between operations: 14.1 us -> 0.64 us
  local copies, waits for them, and re-layouts: 22.3 us -> 9.21 us
  other arithmetic: 12.3 us -> 0 us
    all_gather x2 -> x0, waiting for transfers between devices: 137 us -> none  [the longest x1 98.9 us: local(): lax.all_gather(direction, 'col', axis=0, tiled=True)]
    pallas_call x0 -> x1, Pallas kernels: none -> 92.2 us  [local(): pl.pallas_call(kernel, out_shape=(like(grad), like(grad), like(grad), lik...]
    all_to_all x3 -> x0, blocking collectives: 88.7 us -> none  [the longest x2 70.2 us: copy_for_each(): lax.all_to_all(jnp.broadcast_to(shard[None], (count, *shard.shape)), axis...]
    all_to_all x3 -> x0, waiting for transfers between devices: 39.9 us -> none  [the longest x1 39.9 us: local(): lax.all_to_all(left_cols, 'col', split_axis=0, concat_axis=1, tiled=True)]
    dot_general x4 -> x0, matrix products: 26.1 us -> none  [the longest x1 9.76 us: local(): lax.dot_general(left_cols, turned, (((0,), (0,)), ((), ())), preferred_el...]
    all_to_all x3 -> x0, starting transfers between devices: 21.4 us -> none  [the longest x1 10.7 us: sum_by_axis(): lax.all_to_all(nearer, far, split_axis=0, concat_axis=0, tiled=True)]
    all_to_all x2 -> x0, local copies, waits for them, and re-layouts: 11.2 us -> none  [the longest x1 6.53 us: local(): lax.all_to_all(left_cols, 'col', split_axis=0, concat_axis=1, tiled=True)]
    reduce_sum x2 -> x0, other arithmetic: 9.47 us -> none  [the longest x1 6.79 us: sum_at_owner(): return jnp.sum(pieces, axis=0)]
  transfers between devices with their start and end apart: 5 -> 0, of which waited for: 3 -> 0; matrix products, arithmetic and copies ran while one was open for 15% -> 0% of each run, Pallas kernels for 0% -> 0%
where the time goes in v1:
time: 102 us
  Pallas kernels  92.2 us (90%)
  local copies, waits for them, and re-layouts  9.21 us (9%)
    pallas_call x1, Pallas kernels, local(): pl.pallas_call(kernel, out_shape=(like(grad), like(grad), like(grad), lik...  92.2 us
    unnamed x11, local copies, waits for them, and re-layouts  7.49 us

profile of v1, /device:TPU:4, one launch (start us, length us, event | category | flops | bytes accessed | tf_op | source)
XLA Modules:
  0.0 102.0 jit_solution(9185285677362158225)
XLA Ops:
  0.6 1.7 %copy.12.gram_right = f32[512,64]{1,0:T(8,128)} copy(f32[512,64]{0,1:T(8,128)} %param.13) | data formatting | bytes 262144 | tf_op args[6]
  2.4 92.2 %shard_map.110 = (f32[512,512]{1,0:T(8,128)}, f32[512,512]{1,0:T(8,128)}, f32[512,512]{1,0:T(8,128)}, f32[128,512]{1,0:T(8,128)}, f32[512,64]{1,0:T(8,128)}) custom-call(f32[512,512]{1,0:T(8,128)} %grad.1, f32[512,512]{1,0:T(8,128)} %exp_avg.1, f32[512,512]{1,0:T(8,128)} %exp_avg_sq.1, bf16[128,512]{1,0:T(8,128)(2,1)} %left.1, bf16[64,512]{1,0:T(8,128)(2,1)} %bitcast.1, ...), custom_call_target="tpu_custom_call" | custom-call | tf_op jit(solution)/shard_map/pallas_call | solution.py:392
  94.6 1.7 %copy.13 = f32[512,64]{0,1:T(8,128)} copy(f32[512,64]{1,0:T(8,128)} %get-tuple-element.9) | data formatting | bytes 262144 | tf_op jit(solution)/shard_map/pallas_call | solution.py:392
  96.3 0.0 copy-start.1
  96.3 2.4 %copy.18 = f32[512,512]{1,0:T(8,128)} copy(f32[512,512]{1,0:T(8,128)} %get-tuple-element.15) | data formatting | bytes 2097152
  98.6 0.0 copy-done.1
  98.6 0.0 copy-start
  98.6 1.0 copy.19
  99.6 0.6 copy-done
  100.2 0.0 copy-start.2
  100.2 1.0 copy.20
  101.2 0.1 copy-done.2
  101.3 0.7 copy.21
Async XLA Ops:
  96.3 2.4 %copy-start.1 = (f32[512,512]{1,0:T(8,128)S(1)}, f32[512,512]{1,0:T(8,128)}, u32[]{:S(2)}) copy-start(f32[512,512]{1,0:T(8,128)} %get-tuple-element.16) | copy-start | bytes 3145732
  98.6 1.6 %copy-start = (f32[512,512]{1,0:T(8,128)S(1)}, f32[512,512]{1,0:T(8,128)}, u32[]{:S(2)}) copy-start(f32[512,512]{1,0:T(8,128)} %get-tuple-element.17) | copy-start | bytes 3145732
  100.2 1.1 %copy-start.2 = (f32[128,512]{1,0:T(8,128)S(1)}, f32[128,512]{1,0:T(8,128)}, u32[]{:S(2)}) copy-start(f32[128,512]{1,0:T(8,128)} %get-tuple-element.18) | copy-start | bytes 786436

commit v2 on v1

v2 whole, which is shorter than its diff:
```python
import functools

import jax
import jax.numpy as jnp
from jax import lax
from jax.experimental import pallas as pl
from jax.experimental.pallas import tpu as pltpu
from jax.sharding import PartitionSpec as P

decay = 0.95
bias_fix = 1.0 - decay**10
B16 = jnp.bfloat16
F32 = jnp.float32
BY_ROWS = (((1,), (1,)), ((), ()))
BY_COLS = (((0,), (0,)), ((), ()))
PLAIN = (((1,), (0,)), ((), ()))


def dot(a, b, dims=PLAIN):
    return lax.dot_general(a, b, dims, preferred_element_type=F32)


def kernel(
    grad, exp_avg, exp_avg_sq, left, right_t, gram_left, gram_right,
    update, first, second, left_stat, right_stat,
    grad_v, avg_v, sq_v, gl_v, gr_v, G, R, L, T, LP, EP, rot, right_acc, dirn,
    ER, ES, AO, YB, D1, D1Y, X1, D2, D2Y, D3, S1, S1Y, S2, S2Y, S3,
    in_sem, send_sem, g_sem, r_sem, l_sem, e_sem, er_sem, yb_sem, d1_sem, d1y_sem, x1_sem, d2_sem, d2y_sem, d3_sem,
):
    grp = lax.axis_index("grp")
    col = lax.axis_index("col")
    core = grp % 2
    z = (grp // 2) % 8
    yh = grp // 16
    x = col // 2
    yl = col % 2

    def z_at(k, half=None, c=None):
        h = yh if half is None else half
        cc = core if c is None else c
        return h * 16 + ((z + k + 8) % 8) * 2 + cc

    def c_at(k, flip=0):
        return ((x + k + 4) % 4) * 2 + (yl if flip == 0 else 1 - yl)

    oh = 1 - yh
    oc = 1 - core
    XP = {"grp": grp, "col": c_at(1)}
    XM = {"grp": grp, "col": c_at(-1)}
    YN = {"grp": grp, "col": c_at(0, 1)}
    ZP = {"grp": z_at(1), "col": col}
    ZM = {"grp": z_at(-1), "col": col}
    YF = {"grp": z_at(0, oh), "col": col}
    CO = {"grp": z_at(0, None, oc), "col": col}

    sends = []

    def send(src, dst, sem, to):
        cp = pltpu.make_async_remote_copy(
            src_ref=src, dst_ref=dst, send_sem=send_sem.at[len(sends)], recv_sem=sem,
            device_id=to, device_id_type=pl.DeviceIdType.MESH,
        )
        cp.start()
        sends.append(cp)

    def arrived(dst, sem):
        pltpu.make_async_remote_copy(
            src_ref=dst, dst_ref=dst, send_sem=send_sem.at[0], recv_sem=sem,
            device_id=XP, device_id_type=pl.DeviceIdType.MESH,
        ).wait_recv()

    RB = G.shape[2]
    H = RB // 2
    Q = RB // 4
    W = R.shape[1] // 2

    def g_part(s, q):
        return G.at[s, pl.ds(q * Q, Q)]

    def r_half(s, h):
        return R.at[s, pl.ds(h * W, W)]

    def send_g(s, q, to):
        send(g_part(s, q), g_part(s, q), g_sem.at[s, q], to)

    def send_r(s, h, to):
        send(r_half(s, h), r_half(s, h), r_sem.at[s, h], to)

    def got_g(s, *qs):
        for q in qs:
            arrived(g_part(s, q), g_sem.at[s, q])

    def got_r(s, *hs):
        for h in hs:
            arrived(r_half(s, h), r_sem.at[s, h])

    def send_l(g, to):
        send(L.at[g], L.at[g], l_sem.at[g], to)

    def got_l(g):
        arrived(L.at[g], l_sem.at[g])

    barrier = pltpu.get_barrier_semaphore()
    for to in (XP, XM, YN, ZP, ZM, YF, CO):
        pl.semaphore_signal(barrier, inc=1, device_id=to, device_id_type=pl.DeviceIdType.MESH)
    fetches = []
    for k, (src, dst) in enumerate((
        (grad, grad_v), (right_t, R.at[col]), (left, L.at[grp]),
        (exp_avg, avg_v), (exp_avg_sq, sq_v), (gram_left, gl_v), (gram_right, gr_v),
    )):
        cp = pltpu.make_async_copy(src, dst, in_sem.at[k])
        cp.start()
        fetches.append(cp)
    right_acc[...] = jnp.zeros_like(right_acc)
    rot[...] = jnp.zeros_like(rot)
    fetches[0].wait()
    G[col] = grad_v[...].astype(B16)
    fetches[1].wait()
    fetches[2].wait()
    pl.semaphore_wait(barrier, 7)

    me = col
    xm, xp, yn = c_at(-1), c_at(1), c_at(0, 1)
    far = c_at(2)
    xm_n, xp_n, far_n = c_at(-1, 1), c_at(1, 1), c_at(2, 1)

    for h in (0, 1):
        for to in (YN, XP, XM):
            send_r(me, h, to)
    for to in (ZP, ZM, YF, CO):
        send_l(grp, to)
    send_g(me, 0, XP)
    send_g(me, 3, XM)
    send_g(me, 0, YN)

    def l_pass(g, to):
        got_l(g)
        if to is not None:
            send_l(g, to)
        send_l(g, CO)

    width = right_acc.shape[0]
    picks = lax.broadcasted_iota(jnp.int32, (width, RB), 0)
    lanes = lax.broadcasted_iota(jnp.int32, (width, RB), 1)
    chosen = jnp.where(lanes == picks + col * width, 1.0, 0.0).astype(B16)

    def right_of(s):
        rows = G[s]
        narrow = dot(chosen, rows, BY_ROWS).astype(B16)
        right_acc[...] += dot(narrow, rows)

    def rotate(s):
        rot[...] += dot(L[pl.ds(4 * s, 4)].reshape(RB, RB), T[s], BY_COLS)

    def pair_send(s):
        send(LP.at[pl.ds(2 * s, 2), oc], EP.at[pl.ds(2 * s, 2)], e_sem.at[s], CO)

    order = ((0, 0), (0, 1), (3, 0), (1, 0), (2, 0), (3, 1), (1, 1), (2, 1))

    def over(lo, hi, f):
        def body(i, carry):
            dx = sum(jnp.where(i == n, order[n][0], 0) for n in range(lo, hi))
            flip = sum(jnp.where(i == n, order[n][1], 0) for n in range(lo, hi))
            f(((x + dx) % 4) * 2 + (yl + flip) % 2)
            return carry

        lax.fori_loop(lo, hi, body, 0)

    def rows_of(q):
        return pl.ds(pl.multiple_of(q * Q, Q), Q)

    def half_rows(h):
        return pl.ds(h * H, H)

    def turn_h(s, h):
        T[s, half_rows(h)] = dot(G[s, half_rows(h)], R[...].reshape(RB, RB), BY_ROWS).astype(B16)

    def left_h(s, h):
        LP[2 * s + h] = dot(G[s, half_rows(h)], G[me], BY_ROWS).reshape(2, 128, RB)

    def turn_q(s, q):
        T[s, rows_of(q)] = dot(G[s, rows_of(q)], R[...].reshape(RB, RB), BY_ROWS).astype(B16)

    def left_q(s, q):
        LP[2 * s + q // 2, q % 2] = dot(G[s, rows_of(q)], G[me], BY_ROWS)

    def rotate_q(s, q):
        rot[...] += dot(L[4 * s + q], T[s, rows_of(q)], BY_COLS)

    left_h(me, 0)
    got_r(xm, 0, 1)
    send_r(xm, 0, XP)
    got_r(xp, 0, 1)
    send_r(xp, 1, XM)
    for s in (xm, xp):
        for h in (0, 1):
            send_r(s, h, YN)
    send_g(me, 1, XP)
    send_g(me, 2, XM)
    send_g(me, 1, YN)
    l_pass(z_at(-1), ZP)
    l_pass(z_at(1), ZM)
    g = z_at(0, oh)
    got_l(g)
    send_l(g, ZP)
    send_l(g, ZM)
    send_l(g, CO)
    send_g(me, 2, XP)
    send_g(me, 1, XM)
    got_g(xm, 0)
    send_g(xm, 0, XP)
    got_g(xp, 3)
    send_g(xp, 3, XM)
    left_h(me, 1)
    got_r(far, 0, 1)
    send_r(far, 0, YN)
    send_r(far, 1, YN)
    send_g(me, 2, YN)
    send_g(me, 3, YN)
    pair_send(me)
    l_pass(z_at(-2), ZP)
    l_pass(z_at(2), ZM)
    got_g(xm, 1)
    send_g(xm, 1, XP)
    got_g(xp, 2)
    send_g(xp, 2, XM)
    send_g(me, 3, XP)
    send_g(me, 0, XM)
    for q in (0, 1):
        got_g(yn, q)
        send_g(yn, q, XP)
        send_g(yn, q, XM)
    left_h(yn, 0)
    l_pass(z_at(-1, oh), ZP)
    l_pass(z_at(1, oh), ZM)
    left_h(xm, 0)
    left_h(xp, 1)
    l_pass(z_at(-3), ZP)
    l_pass(z_at(3), None)
    got_r(yn, 0, 1)
    for s in (xm_n, xp_n, far_n):
        got_r(s, 0, 1)
    turn_h(me, 0)
    turn_h(me, 1)
    got_g(yn, 2)
    send_g(yn, 2, XP)
    send_g(yn, 2, XM)
    got_g(far, 0, 3)
    send_g(far, 0, YN)
    send_g(far, 3, YN)
    l_pass(z_at(-2, oh), ZP)
    l_pass(z_at(2, oh), ZM)
    turn_h(yn, 0)
    turn_h(xm, 0)
    turn_h(xp, 1)
    got_g(yn, 3)
    send_g(yn, 3, XP)
    send_g(yn, 3, XM)
    got_g(far, 1, 2)
    send_g(far, 1, YN)
    send_g(far, 2, YN)
    l_pass(z_at(4), None)
    turn_h(yn, 1)
    left_h(yn, 1)
    pair_send(yn)
    for h in (0, 1):
        turn_h(far, h)
        left_h(far, h)
    pair_send(far)
    got_g(xm, 2, 3)
    got_g(xp, 0, 1)
    turn_h(xm, 1)
    left_h(xm, 1)
    l_pass(z_at(-3, oh), None)
    l_pass(z_at(3, oh), ZM)
    turn_h(xp, 0)
    left_h(xp, 0)
    pair_send(xm)
    pair_send(xp)

    far_order = (0, 3, 1, 2)

    def late(n, f):
        def body(i, carry):
            dx = jnp.where(i == 5, 3, jnp.where(i == 6, 1, 2))
            q = jnp.where(i == 7, far_order[n], n)
            f(((x + dx) % 4) * 2 + 1 - yl, q)
            return carry

        lax.fori_loop(5, 8, body, 0)

    def late_got(n):
        got_g(xm_n, n)
        got_g(xp_n, n)
        got_g(far_n, far_order[n])

    for n in (0, 1):
        late_got(n)
        late(n, turn_q)
        late(n, left_q)
    l_pass(z_at(4, oh), None)
    for h in (yh, oh):
        for k in range(8):
            got_l(z_at(k, h, oc))
    over(0, 5, rotate)
    late(0, rotate_q)
    late(1, rotate_q)
    for n in (2, 3):
        late_got(n)
        late(n, turn_q)
        late(n, rotate_q)
        if n == 2:
            late(n, left_q)
    fetches[3].wait()
    fetches[4].wait()

    def moments(i, carry):
        at = pl.ds(i * 64, 64)
        turned = rot[at, :]
        m1 = decay * avg_v[at, :] + (1.0 - decay) * turned
        m2 = decay * sq_v[at, :] + (1.0 - decay) * turned * turned
        first[at, :] = m1
        second[at, :] = m2
        dirn[at, :] = (m1 / bias_fix / (jnp.sqrt(m2 / bias_fix) + 1e-08)).astype(B16)
        return carry

    lax.fori_loop(0, RB // 64, moments, 0)

    E = RB // 8

    def part(d, q, count=1):
        return dot(L[pl.ds(4 * d + q, count)].reshape(count * Q, RB), dirn[...])

    def at_rows(lo, n):
        return pl.ds(lo, n)

    lower, upper, rest, first_e = at_rows(0, H), at_rows(H, H), at_rows(E, H - E), at_rows(0, E)
    quarter = [at_rows(q * Q, Q) for q in range(4)]
    S1[0, lower] = part(xp_n, 0, 2).astype(B16)
    S1[1, lower] = part(xm_n, 0, 2).astype(B16)
    send(S1.at[0, rest], D1.at[0, rest], d1_sem.at[0, 0], XP)
    S1Y[lower] = part(far_n, 0, 2).astype(B16)
    send(S1.at[1, rest], D1.at[1, rest], d1_sem.at[1, 0], XM)
    S1[0, upper] = part(xp_n, 2, 2).astype(B16)
    send(S1Y.at[quarter[0]], D1Y.at[quarter[0]], d1y_sem.at[0], YN)
    S1[1, upper] = part(xm_n, 2, 2).astype(B16)
    send(S1.at[0, upper], D1.at[0, upper], d1_sem.at[0, 1], XP)
    S1Y[upper] = part(far_n, 2, 2).astype(B16)
    send(S1.at[1, upper], D1.at[1, upper], d1_sem.at[1, 1], XM)
    late(3, left_q)
    for q in (2, 1, 3):
        send(S1Y.at[quarter[q]], D1Y.at[quarter[q]], d1y_sem.at[q], YN)
    for d in (0, 1):
        send(S1.at[d, first_e], X1.at[d], x1_sem.at[d], YN)
    for s in (xm_n, xp_n, far_n):
        pair_send(s)
    fetches[5].wait()
    fetches[6].wait()

    def stat_of(half, k):
        b = half * 8 + (z + k + 8) % 8
        return LP[b, core] + EP[b]

    def stat_send(d, k, step):
        length = 4 if d == k else 3
        away = length + 1 - step
        total = stat_of(yh if k == 0 else oh, away if d == 0 else -away)
        if step > 1:
            arrived(ER.at[d, k, step - 2], er_sem.at[d, k, step - 2])
            total = total + ER[d, k, step - 2].astype(F32)
        ES[d, k, step - 1] = total.astype(B16)
        send(
            ES.at[d, k, step - 1], ER.at[d, k, step - 1], er_sem.at[d, k, step - 1],
            ZP if d == 0 else ZM,
        )

    def stat_total(k):
        total = stat_of(yh if k == 0 else oh, 0)
        for d in (0, 1):
            last = 3 if d == k else 2
            arrived(ER.at[d, k, last], er_sem.at[d, k, last])
            total = total + ER[d, k, last].astype(F32)
        return total

    S3[0, upper] = part(xp, 2, 2).astype(B16)
    S3[1, lower] = part(xm, 0, 2).astype(B16)
    for s in (me, xm, xp, yn, far, xm_n, xp_n, far_n):
        arrived(EP.at[pl.ds(2 * s, 2)], e_sem.at[s])
    for k in (1, 0):
        stat_send(0, k, 1)
        stat_send(1, k, 1)

    def second_hop(d, q):
        arrived(D1Y.at[quarter[q]], d1y_sem.at[q])
        own = quarter[q - 2 * d]
        S2[d, own] = (part(far, q) + D1Y[quarter[q]].astype(F32)).astype(B16)
        send(S2.at[d, own], D2.at[d, own], d2_sem.at[d, q - 2 * d], XP if d == 0 else XM)

    over(0, 4, right_of)
    second_hop(0, 0)
    second_hop(1, 2)
    stat_send(0, 1, 2)
    stat_send(1, 1, 2)
    second_hop(0, 1)
    second_hop(1, 3)
    send(S3.at[0, upper], D3.at[0, upper], d3_sem.at[0, 2], XP)
    send(S3.at[1, rest], D3.at[1, rest], d3_sem.at[1, 0], XM)
    stat_send(0, 0, 2)
    stat_send(1, 0, 2)
    for d in (0, 1):
        arrived(D1.at[d, upper], d1_sem.at[d, 1])
        arrived(D1.at[d, rest], d1_sem.at[d, 0])
    S2Y[upper] = (
        part(yn, 2, 2) + D1[0, upper].astype(F32) + D1[1, upper].astype(F32)
    ).astype(B16)
    own = part(yn, 0, 2)
    S2Y[first_e] = own[:E].astype(B16)
    S2Y[rest] = (own[E:] + D1[0, rest].astype(F32) + D1[1, rest].astype(F32)).astype(B16)
    send(S2Y.at[upper], D2Y.at[upper], d2y_sem.at[1], YN)
    send(S2Y.at[lower], D2Y.at[lower], d2y_sem.at[0], YN)
    stat_send(0, 1, 3)
    stat_send(1, 1, 3)
    for d in (0, 1):
        arrived(X1.at[d], x1_sem.at[d])
    S3[1, first_e] = (dot(L[4 * xm, first_e], dirn[...]) + X1[1].astype(F32)).astype(B16)
    send(S3.at[1, first_e], D3.at[1, first_e], d3_sem.at[1, 1], XM)
    arrived(D2.at[0, quarter[0]], d2_sem.at[0, 0])
    own = part(xp, 0) + D2[0, quarter[0]].astype(F32)
    S3[0, first_e] = (own[:E] + X1[0].astype(F32)).astype(B16)
    S3[0, at_rows(E, Q - E)] = own[E:].astype(B16)

    def third_hop(d, q):
        mine = quarter[q - 2 * d]
        arrived(D2.at[d, mine], d2_sem.at[d, q - 2 * d])
        S3[d, quarter[q]] = (
            part(xp if d == 0 else xm, q) + D2[d, mine].astype(F32)
        ).astype(B16)

    def third_send(d, q):
        send(
            S3.at[d, quarter[q]], D3.at[d, quarter[q]], d3_sem.at[d, q],
            XP if d == 0 else XM,
        )

    third_hop(1, 2)
    third_send(0, 0)
    third_send(1, 2)
    stat_send(0, 0, 3)
    third_hop(0, 1)
    third_send(0, 1)
    third_hop(1, 3)
    third_send(1, 3)
    stat_send(1, 1, 4)
    stat_send(1, 0, 3)
    over(4, 8, right_of)
    right_stat[...] = decay * gr_v[...] + (1.0 - decay) * right_acc[...]
    stat_send(0, 0, 4)
    rot[...] = part(me, 0, 4)
    AO[...] = stat_total(1).astype(B16)
    send(AO, YB, yb_sem.at[0], YF)
    left_stat[...] = decay * gl_v[...] + (1.0 - decay) * stat_total(0)
    arrived(D2Y.at[upper], d2y_sem.at[1])
    arrived(D2Y.at[lower], d2y_sem.at[0])
    arrived(D3.at[0, upper], d3_sem.at[0, 2])
    arrived(D3.at[1, rest], d3_sem.at[1, 0])
    arrived(D3.at[1, first_e], d3_sem.at[1, 1])
    rot[upper] += D2Y[upper].astype(F32) + D3[0, upper].astype(F32)
    rot[lower] += D2Y[lower].astype(F32) + D3[1, lower].astype(F32)
    for q in (0, 1):
        arrived(D3.at[0, quarter[q]], d3_sem.at[0, q])
        arrived(D3.at[1, quarter[q + 2]], d3_sem.at[1, q + 2])
    basis = R[...].reshape(RB, RB)
    update[lower] = dot((rot[lower] + D3[0, lower].astype(F32)).astype(B16), basis)
    update[upper] = dot((rot[upper] + D3[1, upper].astype(F32)).astype(B16), basis)
    arrived(YB, yb_sem.at[0])
    left_stat[...] += (1.0 - decay) * YB[...].astype(F32)
    for cp in sends:
        cp.wait_send()


def put_out(*refs):
    held, out, sem = refs[:5], refs[5:10], refs[10]
    copies = [pltpu.make_async_copy(a, b, sem.at[k]) for k, (a, b) in enumerate(zip(held, out))]
    for cp in copies:
        cp.start()
    for cp in copies:
        cp.wait()


def local(grad, exp_avg, exp_avg_sq, left_basis, right_basis, gram_left, gram_right):
    rows, RB = grad.shape
    assert rows == RB
    H = RB // 2
    width = right_basis.shape[1]
    vm = pltpu.VMEM
    dma = pltpu.SemaphoreType.DMA
    scratch = [
        vm((RB, RB), F32), vm((RB, RB), F32), vm((RB, RB), F32), vm((128, RB), F32), vm((width, RB), F32),
        vm((8, RB, RB), B16),
        vm((8, width, RB), B16),
        vm((32, 128, RB), B16),
        vm((8, RB, RB), B16),
        vm((16, 2, 128, RB), F32),
        vm((16, 128, RB), F32),
        vm((RB, RB), F32),
        vm((width, RB), F32),
        vm((RB, RB), B16),
        vm((2, 2, 4, 128, RB), B16),
        vm((2, 2, 4, 128, RB), B16),
        vm((128, RB), B16),
        vm((128, RB), B16),
        vm((2, RB, RB), B16),
        vm((RB, RB), B16),
        vm((2, RB // 8, RB), B16),
        vm((2, H, RB), B16),
        vm((RB, RB), B16),
        vm((2, RB, RB), B16),
        vm((2, RB, RB), B16),
        vm((RB, RB), B16),
        vm((2, H, RB), B16),
        vm((RB, RB), B16),
        vm((2, RB, RB), B16),
        dma((7,)), dma((160,)), dma((8, 4)), dma((8, 2)), dma((32,)), dma((8,)), dma((2, 2, 4)),
        dma((1,)), dma((2, 2)), dma((4,)), dma((2,)), dma((2, 2)), dma((2,)), dma((2, 4)),
    ]
    whole = pl.BlockSpec(memory_space=pl.ANY)
    like = lambda a: pltpu.VMEM(a.shape, F32)
    gram_rt = gram_right.T
    update, first, second, left_stat, right_rt = pl.pallas_call(
        kernel,
        out_shape=(like(grad), like(grad), like(grad), like(gram_left), like(gram_rt)),
        in_specs=[whole] * 7,
        out_specs=(pl.BlockSpec(memory_space=pltpu.VMEM),) * 5,
        scratch_shapes=scratch,
        compiler_params=pltpu.CompilerParams(
            collective_id=0, has_side_effects=True, vmem_limit_bytes=58 * 1024 * 1024
        ),
    )(grad, exp_avg, exp_avg_sq, left_basis, right_basis.T, gram_left, gram_rt)
    results = (update, first, second, left_stat, right_rt)
    update, first, second, left_stat, right_rt = pl.pallas_call(
        put_out,
        out_shape=tuple(jax.ShapeDtypeStruct(a.shape, F32) for a in results),
        in_specs=[pl.BlockSpec(memory_space=pltpu.VMEM)] * 5,
        out_specs=(whole,) * 5,
        scratch_shapes=[dma((5,))],
        compiler_params=pltpu.CompilerParams(vmem_limit_bytes=2 * 1024 * 1024),
    )(*results)
    return update, first, second, left_stat, right_rt.T


def solution(mesh):
    a, b = P("col", "grp"), P("grp", "col")
    return jax.shard_map(
        local, mesh=mesh, in_specs=(a, a, a, b, b, b, b), out_specs=(a, a, a, b, b), check_vma=False
    )
```

time: 102 us -> 86.8 us (0.85); the launches traced: 102 us -> 85.5 us
  local copies, waits for them, and re-layouts: 9.21 us -> 0 us
  Pallas kernels: 92.2 us -> 84.9 us
    pallas_call x1, Pallas kernels: 92.2 us -> 83 us  [local(): pl.pallas_call(kernel, out_shape=(like(grad), like(grad), like(grad), lik...]
    unnamed x11 -> x0, local copies, waits for them, and re-layouts: 7.49 us -> none
    pallas_call x0 -> x1, Pallas kernels: none -> 1.82 us  [local(): pl.pallas_call(put_out, out_shape=tuple((jax.ShapeDtypeStruct(a.shape, F3...]
    pallas_call x1 -> x0, local copies, waits for them, and re-layouts: 1.72 us -> none  [local(): pl.pallas_call(kernel, out_shape=(like(grad), like(grad), like(grad), lik...]
where the time goes in v2:
time: 86.8 us; the launch traced here: 85.5 us
  Pallas kernels  84.9 us (98%)
    pallas_call x1, Pallas kernels, local(): pl.pallas_call(kernel, out_shape=(like(grad), like(grad), like(grad), lik...  83 us
    pallas_call x1, Pallas kernels, local(): pl.pallas_call(put_out, out_shape=tuple((jax.ShapeDtypeStruct(a.shape, F3...  1.82 us

profile of v2, /device:TPU:4, one launch (start us, length us, event | category | flops | bytes accessed | tf_op | source)
XLA Modules:
  0.0 85.5 jit_solution(16988355464130405955)
XLA Ops:
  0.6 83.0 %shard_map.110 = (f32[512,512]{1,0:T(8,128)S(1)}, f32[512,512]{1,0:T(8,128)S(1)}, f32[512,512]{1,0:T(8,128)S(1)}, f32[128,512]{1,0:T(8,128)S(1)}, f32[64,512]{1,0:T(8,128)S(1)}) custom-call(f32[512,512]{1,0:T(8,128)} %grad.1, f32[512,512]{1,0:T(8,128)} %exp_avg.1, f32[512,512]{1,0:T(8,128)} %exp_avg_sq.1, bf16[128,512]{1,0:T(8,128)(2,1)} %left.1, ...), custom_call_target="tpu_custom_call" | custom-call | tf_op jit(solution)/shard_map/pallas_call | solution.py:529
  83.7 1.8 %shard_map.111 = (f32[512,512]{1,0:T(8,128)}, f32[512,512]{1,0:T(8,128)}, f32[512,512]{1,0:T(8,128)}, f32[128,512]{1,0:T(8,128)}, f32[64,512]{1,0:T(8,128)}) custom-call(f32[512,512]{1,0:T(8,128)S(1)} %get-tuple-element.15.refs_0_, f32[512,512]{1,0:T(8,128)S(1)} %get-tuple-element.16.refs_1_, f32[512,512]{1,0:T(8,128)S(1)} %get-tuple-element.17.refs_2_, ...), custom_call_target="tpu_custom_call" | custom-call | tf_op jit(solution)/shard_map/pallas_call | solution.py:540

commit v3 on v2

--- a/solution.py
+++ b/solution.py
@@ -112,7 +112,6 @@
         cp.start()
         fetches.append(cp)
     right_acc[...] = jnp.zeros_like(right_acc)
-    rot[...] = jnp.zeros_like(rot)
     fetches[0].wait()
     G[col] = grad_v[...].astype(B16)
     fetches[1].wait()
@@ -149,9 +148,6 @@
         narrow = dot(chosen, rows, BY_ROWS).astype(B16)
         right_acc[...] += dot(narrow, rows)
 
-    def rotate(s):
-        rot[...] += dot(L[pl.ds(4 * s, 4)].reshape(RB, RB), T[s], BY_COLS)
-
     def pair_send(s):
         send(LP.at[pl.ds(2 * s, 2), oc], EP.at[pl.ds(2 * s, 2)], e_sem.at[s], CO)
 
@@ -183,9 +179,6 @@
 
     def left_q(s, q):
         LP[2 * s + q // 2, q % 2] = dot(G[s, rows_of(q)], G[me], BY_ROWS)
-
-    def rotate_q(s, q):
-        rot[...] += dot(L[4 * s + q], T[s, rows_of(q)], BY_COLS)
 
     left_h(me, 0)
     got_r(xm, 0, 1)
@@ -298,19 +291,18 @@
         late_got(n)
         late(n, turn_q)
         late(n, left_q)
+    late_got(2)
+    late(2, turn_q)
     l_pass(z_at(4, oh), None)
+    late(2, left_q)
+    late_got(3)
+    late(3, turn_q)
     for h in (yh, oh):
         for k in range(8):
             got_l(z_at(k, h, oc))
-    over(0, 5, rotate)
-    late(0, rotate_q)
-    late(1, rotate_q)
-    for n in (2, 3):
-        late_got(n)
-        late(n, turn_q)
-        late(n, rotate_q)
-        if n == 2:
-            late(n, left_q)
+    for h in (0, 1):
+        at = pl.ds(h * H, H)
+        rot[:, at] = dot(L[...].reshape(8 * RB, RB), T[:, :, at].reshape(8 * RB, H), BY_COLS)
     fetches[3].wait()
     fetches[4].wait()
 
@@ -418,6 +410,8 @@
     S2Y[rest] = (own[E:] + D1[0, rest].astype(F32) + D1[1, rest].astype(F32)).astype(B16)
     send(S2Y.at[upper], D2Y.at[upper], d2y_sem.at[1], YN)
     send(S2Y.at[lower], D2Y.at[lower], d2y_sem.at[0], YN)
+    over(4, 8, right_of)
+    right_stat[...] = decay * gr_v[...] + (1.0 - decay) * right_acc[...]
     stat_send(0, 1, 3)
     stat_send(1, 1, 3)
     for d in (0, 1):
@@ -452,12 +446,10 @@
     third_send(1, 3)
     stat_send(1, 1, 4)
     stat_send(1, 0, 3)
-    over(4, 8, right_of)
-    right_stat[...] = decay * gr_v[...] + (1.0 - decay) * right_acc[...]
     stat_send(0, 0, 4)
-    rot[...] = part(me, 0, 4)
     AO[...] = stat_total(1).astype(B16)
     send(AO, YB, yb_sem.at[0], YF)
+    rot[...] = part(me, 0, 4)
     left_stat[...] = decay * gl_v[...] + (1.0 - decay) * stat_total(0)
     arrived(D2Y.at[upper], d2y_sem.at[1])
     arrived(D2Y.at[lower], d2y_sem.at[0])

time: 86.8 us -> 82.2 us (0.947)
  Pallas kernels: 84.9 us -> 80.5 us
    pallas_call x1, Pallas kernels: 83 us -> 78.7 us  [local(): pl.pallas_call(kernel, out_shape=(like(grad), like(grad), like(grad), lik...]
where the time goes in v3:
time: 82.2 us; the launch traced here: 81.3 us
  Pallas kernels  80.5 us (98%)
    pallas_call x1, Pallas kernels, local(): pl.pallas_call(kernel, out_shape=(like(grad), like(grad), like(grad), lik...  78.7 us
    pallas_call x1, Pallas kernels, local(): pl.pallas_call(put_out, out_shape=tuple((jax.ShapeDtypeStruct(a.shape, F3...  1.82 us

profile of v3, /device:TPU:4, one launch (start us, length us, event | category | flops | bytes accessed | tf_op | source)
XLA Modules:
  0.0 81.3 jit_solution(7990190765573832052)
XLA Ops:
  0.6 78.7 %shard_map.110 = (f32[512,512]{1,0:T(8,128)S(1)}, f32[512,512]{1,0:T(8,128)S(1)}, f32[512,512]{1,0:T(8,128)S(1)}, f32[128,512]{1,0:T(8,128)S(1)}, f32[64,512]{1,0:T(8,128)S(1)}) custom-call(f32[512,512]{1,0:T(8,128)} %grad.1, f32[512,512]{1,0:T(8,128)} %exp_avg.1, f32[512,512]{1,0:T(8,128)} %exp_avg_sq.1, bf16[128,512]{1,0:T(8,128)(2,1)} %left.1, ...), custom_call_target="tpu_custom_call" | custom-call | tf_op jit(solution)/shard_map/pallas_call | solution.py:521
  79.3 1.8 %shard_map.111 = (f32[512,512]{1,0:T(8,128)}, f32[512,512]{1,0:T(8,128)}, f32[512,512]{1,0:T(8,128)}, f32[128,512]{1,0:T(8,128)}, f32[64,512]{1,0:T(8,128)}) custom-call(f32[512,512]{1,0:T(8,128)S(1)} %get-tuple-element.15.refs_0_, f32[512,512]{1,0:T(8,128)S(1)} %get-tuple-element.16.refs_1_, f32[512,512]{1,0:T(8,128)S(1)} %get-tuple-element.17.refs_2_, ...), custom_call_target="tpu_custom_call" | custom-call | tf_op jit(solution)/shard_map/pallas_call | solution.py:532
